TPU v7x, 32 devices: a whole 2x2x4 slice. The times are simulated.
32 devices in a mesh: row: 8 (over z, core), col: 4 (over y, x).
Axes of the slice: x: 2, y: 2, z: 4, core: 2. Of those that a mesh axis runs over, the one named last changes fastest.
Arguments:
- queries: bfloat16 [32768, 256], P(('row', 'col')), may hold values from -6 to 6
- documents: bfloat16 [1024, 256], P(('row', 'col')), may hold values from -6 to 6
- log_norms: float32 [32768], P(('row', 'col')), may hold values from 7 to 11
- weights: float32 [32768], P(('row', 'col')), may hold values from 1 to 10
- positives: int32 [32768], P(('row', 'col')), may hold values from 0 to 1023
Outputs:
- grad_queries: bfloat16 [32768, 256], P(('row', 'col'))
- grad_documents: bfloat16 [1024, 256], P(('row', 'col'))
- loss: float32 [], replicated
All inputs are finite; a program needn't handle non-finite values.
Results may differ from a plain program's by a relative error of at most 0.001.
The roundings to bfloat16 on the way count: a program that leaves them out, or rounds other values in their place, can miss the bound.
Values may be sent and summed in bfloat16 or wider, within the bound.
A program may use at most 128 MiB of HBM per device.

v0:
```python
import jax
import jax.numpy as jnp
from jax import lax
from jax.sharding import PartitionSpec as P


def passed_along(block, axis, distance):
    devices = range(lax.axis_size(axis))
    route = [((i - distance) % len(devices), i) for i in devices]
    return lax.ppermute(block, axis, route)


def visit(queries, log_norms, weights, positives, grad_q, pos_scores, block, start):
    count = block.shape[0]
    scores = jnp.dot(queries, block.T, preferred_element_type=jnp.float32) * 0.0625
    probs = jnp.exp(scores - log_norms[:, None])
    doc_ids = start + jnp.arange(count, dtype=jnp.int32)
    hits = (positives[:, None] == doc_ids[None, :]).astype(jnp.float32)
    pos_scores = pos_scores + jnp.sum(hits * scores, axis=1)
    coeffs = ((probs - hits) * weights[:, None]).astype(jnp.bfloat16)
    grad_q = grad_q + jnp.dot(coeffs, block, preferred_element_type=jnp.float32)
    term = lax.dot_general(
        coeffs, queries, (((0,), (0,)), ((), ())), preferred_element_type=jnp.float32
    )
    return (grad_q, pos_scores, term)


def on_device(queries, documents, log_norms, weights, positives):
    n_row = lax.axis_size("row")
    n_col = lax.axis_size("col")
    total_q = queries.shape[0] * n_row * n_col
    width = queries.shape[1]
    grad_q = jnp.zeros(queries.shape, jnp.float32)
    pos_scores = jnp.zeros(log_norms.shape, jnp.float32)
    block = lax.all_gather(documents, "col", axis=0, tiled=True)
    rows_blk = block.shape[0]
    row_index = lax.axis_index("row")

    def turn(step, carry):
        grad_q, pos_scores, block, sums = carry
        start = (row_index - step) % n_row * rows_blk
        grad_q, pos_scores, term = visit(
            queries, log_norms, weights, positives, grad_q, pos_scores, block, start
        )
        sums = sums + term
        block = passed_along(block, "row", 1)
        sums = passed_along(sums, "row", 1)
        return (grad_q, pos_scores, block, sums)

    init = (grad_q, pos_scores, block, jnp.zeros((rows_blk, width), jnp.float32))
    grad_q, pos_scores, block, sums = lax.fori_loop(0, n_row, turn, init)
    grad_d = lax.psum_scatter(sums, "col", scatter_dimension=0, tiled=True)
    local_loss = jnp.sum(weights * (log_norms - pos_scores))
    loss = lax.psum(local_loss, ("row", "col")) / total_q
    grad_queries = (grad_q * 0.0625).astype(jnp.bfloat16)
    grad_documents = (grad_d * 0.0625).astype(jnp.bfloat16)
    return (grad_queries, grad_documents, loss)


def solution(mesh):
    placed = (
        P(("row", "col"), None),
        P(("row", "col"), None),
        P(("row", "col")),
        P(("row", "col")),
        P(("row", "col")),
    )
    return jax.shard_map(
        on_device,
        mesh=mesh,
        in_specs=placed,
        out_specs=(P(("row", "col"), None), P(("row", "col"), None), P()),
        check_vma=False,
    )
```

profile of v0, /device:TPU:0, one launch (start us, length us, event | category | flops | bytes accessed | tf_op | source)
XLA Modules:
  0.0 131.0 jit_solution(2452079206304974767)
XLA Ops:
  7.2 9.9 %all_gather.3 = bf16[128,256]{1,0:T(8,128)(2,1)S(1)} all-gather(bf16[32,256]{1,0:T(8,128)(2,1)} %param.8), channel_id=1, replica_groups=mesh['row'=8,'col'=4] {'col'}, dimensions={0}, use_global_device_ids=true | all-gather | bytes 81920 | tf_op jit(solution)/shard_map/all_gather | solution.py:35
  17.2 0.7 copy-done.2
  17.8 64.5 %while.22 = (s32[]{:T(128)}, f32[1024,256]{1,0:T(8,128)S(1)}, f32[1024]{0:T(1024)S(1)}, bf16[128,256]{1,0:T(8,128)(2,1)S(1)}, f32[128,256]{1,0:T(8,128)S(1)}, /*...) while((s32[]{:T(128)}, f32[1024,256]{1,0:T(8,128)S(1)}, ...), condition=%wide.region_2.3_spmd.clone, body=%wide.region_0.2_spmd.clone.sunk | while | flops 203981968 | bytes 8173965 | solution.py:51
  17.9 1.4 %fusion.23 = (f32[1024]{0:T(1024)S(1)}, f32[1024,128]{0,1:T(8,128)S(1)}) fusion(s32[1024]{0:T(1024)S(1)} %get-tuple-element.408, s32[128]{0:T(128)S(1)} %iota_add_fusion.2, bf16[1024,256]{1,0:T(8,128)(2,1)} %get-tuple-element.406, bf16[128,256]{1,0:T(8,128)(2,1)S(1)} %copy.16), kind=kOutput, calls=%fused_computation.8.clone.1 | convolution fusion | flops 67632128 | bytes 1122816 | tf_op jit(solution)/shard_map/while/body/eval_jaxpr/dot_general | solution.py:15
  19.4 0.3 convolution_add_fusion.5
  19.7 1.7 %collective-permute-start.1 = (f32[128,256]{1,0:T(8,128)S(1)}, f32[128,256]{1,0:T(8,128)S(1)}, u32[]{:S(2)}, u32[]{:S(2)}) collective-permute-start(f32[128,256]{1,0:T(8,128)S(1)} %convolution_add_fusion.5), channel_id=1, source_target_pairs={{28,0},{0,4},{4,8},{8,12},{12,16},{16,20},{20,24},{24,28},{29,1},{... | collective-permute-start | bytes 393224 | tf_op jit(solution)/shard_map/while/body/eval_jaxpr/ppermute | solution.py:10
  21.4 0.6 convolution_add_fusion.4
  22.0 1.4 %collective-permute-done = bf16[128,256]{1,0:T(8,128)(2,1)S(1)} collective-permute-done((bf16[128,256]{1,0:T(8,128)(2,1)S(1)}, bf16[128,256]{1,0:T(8,128)(2,1)S(1)}, u32[]{:S(2)}, u32[]{:S(2)}) %collective-permute-start) | collective-permute-done | bytes 65568 | tf_op jit(solution)/shard_map/while/body/eval_jaxpr/ppermute | solution.py:10
  23.4 2.6 %collective-permute-done.1 = f32[128,256]{1,0:T(8,128)S(1)} collective-permute-done((f32[128,256]{1,0:T(8,128)S(1)}, f32[128,256]{1,0:T(8,128)S(1)}, u32[]{:S(2)}, u32[]{:S(2)}) %collective-permute-start.1) | collective-permute-done | bytes 131104 | tf_op jit(solution)/shard_map/while/body/eval_jaxpr/ppermute | solution.py:10
  26.0 1.4 %fusion.23 = (f32[1024]{0:T(1024)S(1)}, f32[1024,128]{0,1:T(8,128)S(1)}) fusion(s32[1024]{0:T(1024)S(1)} %get-tuple-element.408, s32[128]{0:T(128)S(1)} %iota_add_fusion.2, bf16[1024,256]{1,0:T(8,128)(2,1)} %get-tuple-element.406, bf16[128,256]{1,0:T(8,128)(2,1)S(1)} %copy.16), kind=kOutput, calls=%fused_computation.8.clone.1 | convolution fusion | flops 67632128 | bytes 1122816 | tf_op jit(solution)/shard_map/while/body/eval_jaxpr/dot_general | solution.py:15
  27.4 0.3 convolution_add_fusion.5
  27.8 0.6 convolution_add_fusion.4
  28.4 3.0 %collective-permute-done = bf16[128,256]{1,0:T(8,128)(2,1)S(1)} collective-permute-done((bf16[128,256]{1,0:T(8,128)(2,1)S(1)}, bf16[128,256]{1,0:T(8,128)(2,1)S(1)}, u32[]{:S(2)}, u32[]{:S(2)}) %collective-permute-start) | collective-permute-done | bytes 65568 | tf_op jit(solution)/shard_map/while/body/eval_jaxpr/ppermute | solution.py:10
  31.4 2.6 %collective-permute-done.1 = f32[128,256]{1,0:T(8,128)S(1)} collective-permute-done((f32[128,256]{1,0:T(8,128)S(1)}, f32[128,256]{1,0:T(8,128)S(1)}, u32[]{:S(2)}, u32[]{:S(2)}) %collective-permute-start.1) | collective-permute-done | bytes 131104 | tf_op jit(solution)/shard_map/while/body/eval_jaxpr/ppermute | solution.py:10
  34.1 1.4 %fusion.23 = (f32[1024]{0:T(1024)S(1)}, f32[1024,128]{0,1:T(8,128)S(1)}) fusion(s32[1024]{0:T(1024)S(1)} %get-tuple-element.408, s32[128]{0:T(128)S(1)} %iota_add_fusion.2, bf16[1024,256]{1,0:T(8,128)(2,1)} %get-tuple-element.406, bf16[128,256]{1,0:T(8,128)(2,1)S(1)} %copy.16), kind=kOutput, calls=%fused_computation.8.clone.1 | convolution fusion | flops 67632128 | bytes 1122816 | tf_op jit(solution)/shard_map/while/body/eval_jaxpr/dot_general | solution.py:15
  35.5 0.3 convolution_add_fusion.5
  35.9 0.6 convolution_add_fusion.4
  36.5 3.0 %collective-permute-done = bf16[128,256]{1,0:T(8,128)(2,1)S(1)} collective-permute-done((bf16[128,256]{1,0:T(8,128)(2,1)S(1)}, bf16[128,256]{1,0:T(8,128)(2,1)S(1)}, u32[]{:S(2)}, u32[]{:S(2)}) %collective-permute-start) | collective-permute-done | bytes 65568 | tf_op jit(solution)/shard_map/while/body/eval_jaxpr/ppermute | solution.py:10
  39.5 2.6 %collective-permute-done.1 = f32[128,256]{1,0:T(8,128)S(1)} collective-permute-done((f32[128,256]{1,0:T(8,128)S(1)}, f32[128,256]{1,0:T(8,128)S(1)}, u32[]{:S(2)}, u32[]{:S(2)}) %collective-permute-start.1) | collective-permute-done | bytes 131104 | tf_op jit(solution)/shard_map/while/body/eval_jaxpr/ppermute | solution.py:10
  42.1 1.4 %fusion.23 = (f32[1024]{0:T(1024)S(1)}, f32[1024,128]{0,1:T(8,128)S(1)}) fusion(s32[1024]{0:T(1024)S(1)} %get-tuple-element.408, s32[128]{0:T(128)S(1)} %iota_add_fusion.2, bf16[1024,256]{1,0:T(8,128)(2,1)} %get-tuple-element.406, bf16[128,256]{1,0:T(8,128)(2,1)S(1)} %copy.16), kind=kOutput, calls=%fused_computation.8.clone.1 | convolution fusion | flops 67632128 | bytes 1122816 | tf_op jit(solution)/shard_map/while/body/eval_jaxpr/dot_general | solution.py:15
  43.6 0.3 convolution_add_fusion.5
  44.0 0.6 convolution_add_fusion.4
  44.6 3.0 %collective-permute-done = bf16[128,256]{1,0:T(8,128)(2,1)S(1)} collective-permute-done((bf16[128,256]{1,0:T(8,128)(2,1)S(1)}, bf16[128,256]{1,0:T(8,128)(2,1)S(1)}, u32[]{:S(2)}, u32[]{:S(2)}) %collective-permute-start) | collective-permute-done | bytes 65568 | tf_op jit(solution)/shard_map/while/body/eval_jaxpr/ppermute | solution.py:10
  47.6 2.6 %collective-permute-done.1 = f32[128,256]{1,0:T(8,128)S(1)} collective-permute-done((f32[128,256]{1,0:T(8,128)S(1)}, f32[128,256]{1,0:T(8,128)S(1)}, u32[]{:S(2)}, u32[]{:S(2)}) %collective-permute-start.1) | collective-permute-done | bytes 131104 | tf_op jit(solution)/shard_map/while/body/eval_jaxpr/ppermute | solution.py:10
  50.2 1.4 %fusion.23 = (f32[1024]{0:T(1024)S(1)}, f32[1024,128]{0,1:T(8,128)S(1)}) fusion(s32[1024]{0:T(1024)S(1)} %get-tuple-element.408, s32[128]{0:T(128)S(1)} %iota_add_fusion.2, bf16[1024,256]{1,0:T(8,128)(2,1)} %get-tuple-element.406, bf16[128,256]{1,0:T(8,128)(2,1)S(1)} %copy.16), kind=kOutput, calls=%fused_computation.8.clone.1 | convolution fusion | flops 67632128 | bytes 1122816 | tf_op jit(solution)/shard_map/while/body/eval_jaxpr/dot_general | solution.py:15
  51.6 0.3 convolution_add_fusion.5
  52.0 0.6 convolution_add_fusion.4
  52.6 3.0 %collective-permute-done = bf16[128,256]{1,0:T(8,128)(2,1)S(1)} collective-permute-done((bf16[128,256]{1,0:T(8,128)(2,1)S(1)}, bf16[128,256]{1,0:T(8,128)(2,1)S(1)}, u32[]{:S(2)}, u32[]{:S(2)}) %collective-permute-start) | collective-permute-done | bytes 65568 | tf_op jit(solution)/shard_map/while/body/eval_jaxpr/ppermute | solution.py:10
  55.6 2.6 %collective-permute-done.1 = f32[128,256]{1,0:T(8,128)S(1)} collective-permute-done((f32[128,256]{1,0:T(8,128)S(1)}, f32[128,256]{1,0:T(8,128)S(1)}, u32[]{:S(2)}, u32[]{:S(2)}) %collective-permute-start.1) | collective-permute-done | bytes 131104 | tf_op jit(solution)/shard_map/while/body/eval_jaxpr/ppermute | solution.py:10
  58.3 1.4 %fusion.23 = (f32[1024]{0:T(1024)S(1)}, f32[1024,128]{0,1:T(8,128)S(1)}) fusion(s32[1024]{0:T(1024)S(1)} %get-tuple-element.408, s32[128]{0:T(128)S(1)} %iota_add_fusion.2, bf16[1024,256]{1,0:T(8,128)(2,1)} %get-tuple-element.406, bf16[128,256]{1,0:T(8,128)(2,1)S(1)} %copy.16), kind=kOutput, calls=%fused_computation.8.clone.1 | convolution fusion | flops 67632128 | bytes 1122816 | tf_op jit(solution)/shard_map/while/body/eval_jaxpr/dot_general | solution.py:15
  59.7 0.3 convolution_add_fusion.5
  60.1 0.6 convolution_add_fusion.4
  60.7 3.0 %collective-permute-done = bf16[128,256]{1,0:T(8,128)(2,1)S(1)} collective-permute-done((bf16[128,256]{1,0:T(8,128)(2,1)S(1)}, bf16[128,256]{1,0:T(8,128)(2,1)S(1)}, u32[]{:S(2)}, u32[]{:S(2)}) %collective-permute-start) | collective-permute-done | bytes 65568 | tf_op jit(solution)/shard_map/while/body/eval_jaxpr/ppermute | solution.py:10
  63.7 2.6 %collective-permute-done.1 = f32[128,256]{1,0:T(8,128)S(1)} collective-permute-done((f32[128,256]{1,0:T(8,128)S(1)}, f32[128,256]{1,0:T(8,128)S(1)}, u32[]{:S(2)}, u32[]{:S(2)}) %collective-permute-start.1) | collective-permute-done | bytes 131104 | tf_op jit(solution)/shard_map/while/body/eval_jaxpr/ppermute | solution.py:10
  66.3 1.4 %fusion.23 = (f32[1024]{0:T(1024)S(1)}, f32[1024,128]{0,1:T(8,128)S(1)}) fusion(s32[1024]{0:T(1024)S(1)} %get-tuple-element.408, s32[128]{0:T(128)S(1)} %iota_add_fusion.2, bf16[1024,256]{1,0:T(8,128)(2,1)} %get-tuple-element.406, bf16[128,256]{1,0:T(8,128)(2,1)S(1)} %copy.16), kind=kOutput, calls=%fused_computation.8.clone.1 | convolution fusion | flops 67632128 | bytes 1122816 | tf_op jit(solution)/shard_map/while/body/eval_jaxpr/dot_general | solution.py:15
  67.8 0.3 convolution_add_fusion.5
  68.1 0.6 convolution_add_fusion.4
  68.7 3.0 %collective-permute-done = bf16[128,256]{1,0:T(8,128)(2,1)S(1)} collective-permute-done((bf16[128,256]{1,0:T(8,128)(2,1)S(1)}, bf16[128,256]{1,0:T(8,128)(2,1)S(1)}, u32[]{:S(2)}, u32[]{:S(2)}) %collective-permute-start) | collective-permute-done | bytes 65568 | tf_op jit(solution)/shard_map/while/body/eval_jaxpr/ppermute | solution.py:10
  71.8 2.6 %collective-permute-done.1 = f32[128,256]{1,0:T(8,128)S(1)} collective-permute-done((f32[128,256]{1,0:T(8,128)S(1)}, f32[128,256]{1,0:T(8,128)S(1)}, u32[]{:S(2)}, u32[]{:S(2)}) %collective-permute-start.1) | collective-permute-done | bytes 131104 | tf_op jit(solution)/shard_map/while/body/eval_jaxpr/ppermute | solution.py:10
  74.4 1.4 %fusion.23 = (f32[1024]{0:T(1024)S(1)}, f32[1024,128]{0,1:T(8,128)S(1)}) fusion(s32[1024]{0:T(1024)S(1)} %get-tuple-element.408, s32[128]{0:T(128)S(1)} %iota_add_fusion.2, bf16[1024,256]{1,0:T(8,128)(2,1)} %get-tuple-element.406, bf16[128,256]{1,0:T(8,128)(2,1)S(1)} %copy.16), kind=kOutput, calls=%fused_computation.8.clone.1 | convolution fusion | flops 67632128 | bytes 1122816 | tf_op jit(solution)/shard_map/while/body/eval_jaxpr/dot_general | solution.py:15
  75.8 0.3 convolution_add_fusion.5
  76.2 0.6 convolution_add_fusion.4
  76.8 3.0 %collective-permute-done = bf16[128,256]{1,0:T(8,128)(2,1)S(1)} collective-permute-done((bf16[128,256]{1,0:T(8,128)(2,1)S(1)}, bf16[128,256]{1,0:T(8,128)(2,1)S(1)}, u32[]{:S(2)}, u32[]{:S(2)}) %collective-permute-start) | collective-permute-done | bytes 65568 | tf_op jit(solution)/shard_map/while/body/eval_jaxpr/ppermute | solution.py:10
  79.8 2.6 %collective-permute-done.1 = f32[128,256]{1,0:T(8,128)S(1)} collective-permute-done((f32[128,256]{1,0:T(8,128)S(1)}, f32[128,256]{1,0:T(8,128)S(1)}, u32[]{:S(2)}, u32[]{:S(2)}) %collective-permute-start.1) | collective-permute-done | bytes 131104 | tf_op jit(solution)/shard_map/while/body/eval_jaxpr/ppermute | solution.py:10
  82.4 0.6 multiply_reduce_fusion
  83.1 37.1 %psum.7 = f32[]{:T(128)} all-reduce(f32[]{:T(128)} %multiply_reduce_fusion), channel_id=1, replica_groups=mesh['row'=8,'col'=4] {'row','col'}, use_global_device_ids=true, to_apply=%region_5.6 | all-reduce | flops 1 | bytes 8 | tf_op jit(solution)/shard_map/psum | solution.py:54
  120.8 0.9 multiply_convert_fusion
  121.7 1.4 %multiply_convert_fusion.1 = bf16[32,256]{1,0:T(8,128)(2,1)} fusion(f32[32,256]{1,0:T(8,128)} %reduce-scatter.2.cloned.1.call-done), kind=kLoop, calls=%fused_computation.12 | loop fusion | flops 16384 | bytes 49152 | tf_op jit(solution)/shard_map/convert_element_type | solution.py:56
  (68 shorter events, 0.8 us)
Async XLA Ops:
  7.2 114.5 %reduce-scatter.2.cloned.1.call-start = ((), (), s32[]{:S(2)}) async-start(), calls=%async_computation.1 | async-start | bytes 163840 | tf_op jit(solution)/shard_map/reduce_scatter | solution.py:52
  17.1 0.7 copy-start.2
  17.1 0.7 copy-start.3
  17.1 0.7 copy-start.4
  17.8 5.5 %collective-permute-start = (bf16[128,256]{1,0:T(8,128)(2,1)S(1)}, bf16[128,256]{1,0:T(8,128)(2,1)S(1)}, u32[]{:S(2)}, u32[]{:S(2)}) collective-permute-start(bf16[128,256]{1,0:T(8,128)(2,1)S(1)} %copy.16), channel_id=1, source_target_pairs={{28,0},{0,4},{4,8},{8,12},{12,16},{16,20},{20,24},{24,28},{29,1},{... | collective-permute-start | bytes 196616 | tf_op jit(solution)/shard_map/while/body/eval_jaxpr/ppermute | solution.py:10
  17.9 1.4 %copy-start = (bf16[1024,256]{1,0:T(8,128)(2,1)S(1)}, bf16[1024,256]{1,0:T(8,128)(2,1)}, u32[]{:S(2)}) copy-start(bf16[1024,256]{1,0:T(8,128)(2,1)} %get-tuple-element.406) | copy-start | bytes 1572868 | tf_op jit(solution)/shard_map/while
  19.7 6.2 %collective-permute-start.1 = (f32[128,256]{1,0:T(8,128)S(1)}, f32[128,256]{1,0:T(8,128)S(1)}, u32[]{:S(2)}, u32[]{:S(2)}) collective-permute-start(f32[128,256]{1,0:T(8,128)S(1)} %convolution_add_fusion.5), channel_id=1, source_target_pairs={{28,0},{0,4},{4,8},{8,12},{12,16},{16,20},{20,24},{24,28},{29,1},{... | collective-permute-start | bytes 393224 | tf_op jit(solution)/shard_map/while/body/eval_jaxpr/ppermute | solution.py:10
  26.0 5.5 %collective-permute-start = (bf16[128,256]{1,0:T(8,128)(2,1)S(1)}, bf16[128,256]{1,0:T(8,128)(2,1)S(1)}, u32[]{:S(2)}, u32[]{:S(2)}) collective-permute-start(bf16[128,256]{1,0:T(8,128)(2,1)S(1)} %copy.16), channel_id=1, source_target_pairs={{28,0},{0,4},{4,8},{8,12},{12,16},{16,20},{20,24},{24,28},{29,1},{... | collective-permute-start | bytes 196616 | tf_op jit(solution)/shard_map/while/body/eval_jaxpr/ppermute | solution.py:10
  26.0 1.4 %copy-start = (bf16[1024,256]{1,0:T(8,128)(2,1)S(1)}, bf16[1024,256]{1,0:T(8,128)(2,1)}, u32[]{:S(2)}) copy-start(bf16[1024,256]{1,0:T(8,128)(2,1)} %get-tuple-element.406) | copy-start | bytes 1572868 | tf_op jit(solution)/shard_map/while
  27.8 6.2 %collective-permute-start.1 = (f32[128,256]{1,0:T(8,128)S(1)}, f32[128,256]{1,0:T(8,128)S(1)}, u32[]{:S(2)}, u32[]{:S(2)}) collective-permute-start(f32[128,256]{1,0:T(8,128)S(1)} %convolution_add_fusion.5), channel_id=1, source_target_pairs={{28,0},{0,4},{4,8},{8,12},{12,16},{16,20},{20,24},{24,28},{29,1},{... | collective-permute-start | bytes 393224 | tf_op jit(solution)/shard_map/while/body/eval_jaxpr/ppermute | solution.py:10
  34.0 5.5 %collective-permute-start = (bf16[128,256]{1,0:T(8,128)(2,1)S(1)}, bf16[128,256]{1,0:T(8,128)(2,1)S(1)}, u32[]{:S(2)}, u32[]{:S(2)}) collective-permute-start(bf16[128,256]{1,0:T(8,128)(2,1)S(1)} %copy.16), channel_id=1, source_target_pairs={{28,0},{0,4},{4,8},{8,12},{12,16},{16,20},{20,24},{24,28},{29,1},{... | collective-permute-start | bytes 196616 | tf_op jit(solution)/shard_map/while/body/eval_jaxpr/ppermute | solution.py:10
  34.1 1.4 %copy-start = (bf16[1024,256]{1,0:T(8,128)(2,1)S(1)}, bf16[1024,256]{1,0:T(8,128)(2,1)}, u32[]{:S(2)}) copy-start(bf16[1024,256]{1,0:T(8,128)(2,1)} %get-tuple-element.406) | copy-start | bytes 1572868 | tf_op jit(solution)/shard_map/while
  35.8 6.2 %collective-permute-start.1 = (f32[128,256]{1,0:T(8,128)S(1)}, f32[128,256]{1,0:T(8,128)S(1)}, u32[]{:S(2)}, u32[]{:S(2)}) collective-permute-start(f32[128,256]{1,0:T(8,128)S(1)} %convolution_add_fusion.5), channel_id=1, source_target_pairs={{28,0},{0,4},{4,8},{8,12},{12,16},{16,20},{20,24},{24,28},{29,1},{... | collective-permute-start | bytes 393224 | tf_op jit(solution)/shard_map/while/body/eval_jaxpr/ppermute | solution.py:10
  42.1 5.5 %collective-permute-start = (bf16[128,256]{1,0:T(8,128)(2,1)S(1)}, bf16[128,256]{1,0:T(8,128)(2,1)S(1)}, u32[]{:S(2)}, u32[]{:S(2)}) collective-permute-start(bf16[128,256]{1,0:T(8,128)(2,1)S(1)} %copy.16), channel_id=1, source_target_pairs={{28,0},{0,4},{4,8},{8,12},{12,16},{16,20},{20,24},{24,28},{29,1},{... | collective-permute-start | bytes 196616 | tf_op jit(solution)/shard_map/while/body/eval_jaxpr/ppermute | solution.py:10
  42.1 1.4 %copy-start = (bf16[1024,256]{1,0:T(8,128)(2,1)S(1)}, bf16[1024,256]{1,0:T(8,128)(2,1)}, u32[]{:S(2)}) copy-start(bf16[1024,256]{1,0:T(8,128)(2,1)} %get-tuple-element.406) | copy-start | bytes 1572868 | tf_op jit(solution)/shard_map/while
  43.9 6.2 %collective-permute-start.1 = (f32[128,256]{1,0:T(8,128)S(1)}, f32[128,256]{1,0:T(8,128)S(1)}, u32[]{:S(2)}, u32[]{:S(2)}) collective-permute-start(f32[128,256]{1,0:T(8,128)S(1)} %convolution_add_fusion.5), channel_id=1, source_target_pairs={{28,0},{0,4},{4,8},{8,12},{12,16},{16,20},{20,24},{24,28},{29,1},{... | collective-permute-start | bytes 393224 | tf_op jit(solution)/shard_map/while/body/eval_jaxpr/ppermute | solution.py:10
  50.1 5.5 %collective-permute-start = (bf16[128,256]{1,0:T(8,128)(2,1)S(1)}, bf16[128,256]{1,0:T(8,128)(2,1)S(1)}, u32[]{:S(2)}, u32[]{:S(2)}) collective-permute-start(bf16[128,256]{1,0:T(8,128)(2,1)S(1)} %copy.16), channel_id=1, source_target_pairs={{28,0},{0,4},{4,8},{8,12},{12,16},{16,20},{20,24},{24,28},{29,1},{... | collective-permute-start | bytes 196616 | tf_op jit(solution)/shard_map/while/body/eval_jaxpr/ppermute | solution.py:10
  50.2 1.4 %copy-start = (bf16[1024,256]{1,0:T(8,128)(2,1)S(1)}, bf16[1024,256]{1,0:T(8,128)(2,1)}, u32[]{:S(2)}) copy-start(bf16[1024,256]{1,0:T(8,128)(2,1)} %get-tuple-element.406) | copy-start | bytes 1572868 | tf_op jit(solution)/shard_map/while
  52.0 6.2 %collective-permute-start.1 = (f32[128,256]{1,0:T(8,128)S(1)}, f32[128,256]{1,0:T(8,128)S(1)}, u32[]{:S(2)}, u32[]{:S(2)}) collective-permute-start(f32[128,256]{1,0:T(8,128)S(1)} %convolution_add_fusion.5), channel_id=1, source_target_pairs={{28,0},{0,4},{4,8},{8,12},{12,16},{16,20},{20,24},{24,28},{29,1},{... | collective-permute-start | bytes 393224 | tf_op jit(solution)/shard_map/while/body/eval_jaxpr/ppermute | solution.py:10
  58.2 5.5 %collective-permute-start = (bf16[128,256]{1,0:T(8,128)(2,1)S(1)}, bf16[128,256]{1,0:T(8,128)(2,1)S(1)}, u32[]{:S(2)}, u32[]{:S(2)}) collective-permute-start(bf16[128,256]{1,0:T(8,128)(2,1)S(1)} %copy.16), channel_id=1, source_target_pairs={{28,0},{0,4},{4,8},{8,12},{12,16},{16,20},{20,24},{24,28},{29,1},{... | collective-permute-start | bytes 196616 | tf_op jit(solution)/shard_map/while/body/eval_jaxpr/ppermute | solution.py:10
  58.2 1.4 %copy-start = (bf16[1024,256]{1,0:T(8,128)(2,1)S(1)}, bf16[1024,256]{1,0:T(8,128)(2,1)}, u32[]{:S(2)}) copy-start(bf16[1024,256]{1,0:T(8,128)(2,1)} %get-tuple-element.406) | copy-start | bytes 1572868 | tf_op jit(solution)/shard_map/while
  60.0 6.2 %collective-permute-start.1 = (f32[128,256]{1,0:T(8,128)S(1)}, f32[128,256]{1,0:T(8,128)S(1)}, u32[]{:S(2)}, u32[]{:S(2)}) collective-permute-start(f32[128,256]{1,0:T(8,128)S(1)} %convolution_add_fusion.5), channel_id=1, source_target_pairs={{28,0},{0,4},{4,8},{8,12},{12,16},{16,20},{20,24},{24,28},{29,1},{... | collective-permute-start | bytes 393224 | tf_op jit(solution)/shard_map/while/body/eval_jaxpr/ppermute | solution.py:10
  66.3 5.5 %collective-permute-start = (bf16[128,256]{1,0:T(8,128)(2,1)S(1)}, bf16[128,256]{1,0:T(8,128)(2,1)S(1)}, u32[]{:S(2)}, u32[]{:S(2)}) collective-permute-start(bf16[128,256]{1,0:T(8,128)(2,1)S(1)} %copy.16), channel_id=1, source_target_pairs={{28,0},{0,4},{4,8},{8,12},{12,16},{16,20},{20,24},{24,28},{29,1},{... | collective-permute-start | bytes 196616 | tf_op jit(solution)/shard_map/while/body/eval_jaxpr/ppermute | solution.py:10
  66.3 1.4 %copy-start = (bf16[1024,256]{1,0:T(8,128)(2,1)S(1)}, bf16[1024,256]{1,0:T(8,128)(2,1)}, u32[]{:S(2)}) copy-start(bf16[1024,256]{1,0:T(8,128)(2,1)} %get-tuple-element.406) | copy-start | bytes 1572868 | tf_op jit(solution)/shard_map/while
  68.1 6.2 %collective-permute-start.1 = (f32[128,256]{1,0:T(8,128)S(1)}, f32[128,256]{1,0:T(8,128)S(1)}, u32[]{:S(2)}, u32[]{:S(2)}) collective-permute-start(f32[128,256]{1,0:T(8,128)S(1)} %convolution_add_fusion.5), channel_id=1, source_target_pairs={{28,0},{0,4},{4,8},{8,12},{12,16},{16,20},{20,24},{24,28},{29,1},{... | collective-permute-start | bytes 393224 | tf_op jit(solution)/shard_map/while/body/eval_jaxpr/ppermute | solution.py:10
  74.3 5.5 %collective-permute-start = (bf16[128,256]{1,0:T(8,128)(2,1)S(1)}, bf16[128,256]{1,0:T(8,128)(2,1)S(1)}, u32[]{:S(2)}, u32[]{:S(2)}) collective-permute-start(bf16[128,256]{1,0:T(8,128)(2,1)S(1)} %copy.16), channel_id=1, source_target_pairs={{28,0},{0,4},{4,8},{8,12},{12,16},{16,20},{20,24},{24,28},{29,1},{... | collective-permute-start | bytes 196616 | tf_op jit(solution)/shard_map/while/body/eval_jaxpr/ppermute | solution.py:10
  74.4 1.4 %copy-start = (bf16[1024,256]{1,0:T(8,128)(2,1)S(1)}, bf16[1024,256]{1,0:T(8,128)(2,1)}, u32[]{:S(2)}) copy-start(bf16[1024,256]{1,0:T(8,128)(2,1)} %get-tuple-element.406) | copy-start | bytes 1572868 | tf_op jit(solution)/shard_map/while
  76.1 6.2 %collective-permute-start.1 = (f32[128,256]{1,0:T(8,128)S(1)}, f32[128,256]{1,0:T(8,128)S(1)}, u32[]{:S(2)}, u32[]{:S(2)}) collective-permute-start(f32[128,256]{1,0:T(8,128)S(1)} %convolution_add_fusion.5), channel_id=1, source_target_pairs={{28,0},{0,4},{4,8},{8,12},{12,16},{16,20},{20,24},{24,28},{29,1},{... | collective-permute-start | bytes 393224 | tf_op jit(solution)/shard_map/while/body/eval_jaxpr/ppermute | solution.py:10
  82.4 0.7 copy-start.1
Sparse Core Ops, SparseCore 0:
  83.2 21.3 reduce-scatter.1
where the time goes:
time: 132 us; the launch traced here: 131 us
  blocking collectives  47 us (36%)
  waiting for transfers between devices  43 us (33%)
  matrix products  18.5 us (14%)
  between operations  15.9 us (12%)
  other arithmetic  2.93 us (2%)
  starting transfers between devices  2.21 us (2%)
    ppermute x16, waiting for transfers between devices, passed_along(): return lax.ppermute(block, axis, route)  42.9 us
    psum x1, blocking collectives, on_device(): loss = lax.psum(local_loss, ('row', 'col')) / total_q  37.1 us
    dot_general x8, matrix products, visit(): jnp.dot(queries, block.T, preferred_element_type=jnp.float32) * 0.0625  11.4 us
    all_gather x1, blocking collectives, on_device(): block = lax.all_gather(documents, 'col', axis=0, tiled=True)  9.88 us
    dot_general x8, matrix products, visit(): grad_q = grad_q + jnp.dot(coeffs, block, preferred_element_type=jnp.float32)  4.62 us
  transfers between devices with their start and end apart: 17, of which 16 were waited for; matrix products, arithmetic and copies ran while one was open for 15% of the time, Pallas kernels for 0%

commit v1 on v0

v1 whole, which is shorter than its diff:
```python
import functools
import math

import jax
import jax.numpy as jnp
from jax import lax
from jax.experimental import pallas as pl
from jax.experimental.pallas import tpu as pltpu
from jax.sharding import PartitionSpec as P

MESH = pl.DeviceIdType.MESH
LOG2E = math.log2(math.e)
F32 = jnp.float32
BF16 = jnp.bfloat16


def flipped(index, step, size):
    total, bit = 0, 1
    while bit < size:
        own = (index // bit) % 2
        other = (step // bit) % 2
        total = total + bit * ((own + other) % 2)
        bit *= 2
    return total


def tree_sum(parts):
    while len(parts) > 1:
        parts = [parts[i] + parts[i + 1] for i in range(0, len(parts), 2)]
    return parts[0]


def kernel(
    n_row, n_col, nd_own, total_q,
    q_hbm, d_hbm, ln_ref, w_ref, pos_ref,
    gq_ref, gd_ref, loss_ref,
    q, q_t, docs, coeffs, part, recv1, recv2, recv3, bias,
    loss_own, loss_in1, loss_in2, loss_in3,
    local_sem, s_z, r_z, s_p, r_p, s_c, r_c, s_f, r_f,
    s_1, r_1, s_2, r_2, s_3, r_3, s_l, r_l,
):
    chips = n_row // 2
    row = lax.axis_index("row")
    col = lax.axis_index("col")
    core = row % 2
    chip = row // 2
    nq, width = q.shape
    half = chips * nd_own
    block = 2 * half

    partner = (chip * 2 + (1 - core), col)
    along_row = [None] + [(flipped(chip, t, chips) * 2 + core, col) for t in range(1, chips)]
    along_col = [None] + [(row, flipped(col, s, n_col)) for s in range(1, n_col)]

    get_d = pltpu.make_async_copy(d_hbm, docs.at[pl.ds(0, nd_own)], local_sem.at[0])
    get_d.start()
    get_q = pltpu.make_async_copy(q_hbm, q, local_sem.at[1])
    get_q.start()

    barrier = pltpu.get_barrier_semaphore()
    peers = [partner] + along_row[1:] + along_col[1:]
    for peer in peers:
        pl.semaphore_signal(barrier, inc=1, device_id=peer, device_id_type=MESH)
    get_d.wait()
    pl.semaphore_wait(barrier, len(peers))

    def send(src, dst, s_sem, r_sem, peer):
        return pltpu.make_async_remote_copy(
            src_ref=src, dst_ref=dst, send_sem=s_sem, recv_sem=r_sem,
            device_id=peer, device_id_type=MESH,
        )

    def piece(s, k, t, count=1):
        return docs.at[pl.ds(s * block + k * half + t * nd_own, count * nd_own)]

    started = []

    def go(copy):
        copy.start()
        started.append(copy)
        return copy

    z_copies = [None]
    for t in range(1, chips):
        z_copies.append(go(send(piece(0, 0, 0), piece(0, 0, t), s_z.at[t], r_z.at[t], along_row[t])))
    for t in range(chips):
        if t:
            z_copies[t].wait_recv()
        for s in range(1, n_col):
            send(piece(0, 0, t), piece(s, 0, t), s_c.at[s], r_c.at[s], along_col[s]).start()
        if t == 0:
            bias[...] = ln_ref[...] * LOG2E - jnp.log2(w_ref[...])
            get_q.wait()
            q_t[...] = q[...].T
    own_fwd = [
        go(send(piece(0, 0, 0, chips), piece(0, 1, 0, chips), s_f.at[0], r_f.at[0], partner))
    ]

    rows_per = math.gcd(block, 256)
    pieces = rows_per // nd_own
    iota = lax.broadcasted_iota(jnp.int32, (nd_own, nq), 0)

    def scores_of(s, sub, acc):
        base = pl.multiple_of(s * block + sub * rows_per, rows_per)
        d = docs[pl.ds(base, rows_per), :]
        sc = jnp.dot(d, q_t[...], preferred_element_type=F32)
        other_col = flipped(col, s, n_col)
        for p in range(pieces):
            at = sub * pieces + p
            k, t = at // chips, at % chips
            owner_row = flipped(chip, t, chips) * 2 + (core + k) % 2
            first = (owner_row * n_col + other_col) * nd_own
            x = sc[p * nd_own:(p + 1) * nd_own, :]
            hit_w = jnp.where(pos_ref[...] - first == iota, w_ref[...], 0.0)
            co = jnp.exp2(x * (0.0625 * LOG2E) - bias[...]) - hit_w
            coeffs[pl.ds(base + p * nd_own, nd_own), :] = co.astype(BF16)
            acc = acc + hit_w * x
        part[pl.ds(base, rows_per), :] = jnp.dot(
            coeffs[pl.ds(base, rows_per), :], q[...], preferred_element_type=F32
        )
        return acc

    n_sub = block // rows_per
    hit_sum = jnp.zeros((nd_own, nq), F32)
    firsts = []

    def own_half(s):
        return part.at[pl.ds(s * block, half)]

    def reduce_pair(s):
        firsts[s].wait_recv()
        own = pl.ds(s * block, half)
        part[own, :] = part[own, :] + recv1[pl.ds(s * half, half), :]
        if s:
            seconds.append(
                go(send(own_half(s), recv2.at[pl.ds(s * half, half)], s_2.at[s], r_2.at[s], along_col[s]))
            )

    seconds = [None]
    fwd = own_fwd
    for s in range(n_col):
        if s:
            whole = send(piece(0, 0, 0, chips), piece(s, 0, 0, chips), s_c.at[s], r_c.at[s], along_col[s])
            whole.wait_recv()
            fwd.append(
                go(send(piece(s, 0, 0, chips), piece(s, 1, 0, chips), s_f.at[s], r_f.at[s], partner))
            )
        fwd[s].wait_recv()
        if n_sub == 1:
            hit_sum = scores_of(s, 0, hit_sum)
        else:
            hit_sum = lax.fori_loop(0, n_sub, functools.partial(scores_of, s), hit_sum)
        firsts.append(
            go(send(
                part.at[pl.ds(s * block + half, half)], recv1.at[pl.ds(s * half, half)],
                s_1.at[s], r_1.at[s], partner,
            ))
        )
        if s:
            reduce_pair(s - 1)

    terms = w_ref[...] * ln_ref[...] - 0.0625 * jnp.sum(hit_sum, axis=0, keepdims=True)
    loss_own[0] = jnp.broadcast_to(jnp.sum(terms, axis=1, keepdims=True), (8, 128))
    l1 = go(send(loss_own.at[0], loss_in1.at[1], s_l.at[0], r_l.at[0], partner))
    reduce_pair(n_col - 1)
    l1.wait_recv()
    loss_own[1] = loss_own[0] + loss_in1[1]
    l2 = [go(send(loss_own.at[1], loss_in2.at[s], s_l.at[s], r_l.at[s], along_col[s])) for s in range(1, n_col)]

    d_t = docs[...].T
    chunk = math.gcd(nq, 256)
    n_chunks = nq // chunk

    def query_gradient(j):
        at = slice(j * chunk, (j + 1) * chunk)
        g = jnp.dot(d_t, coeffs[:, at], preferred_element_type=F32)
        gq_ref[at, :] = (g.T * 0.0625).astype(BF16)

    for j in range(n_chunks):
        query_gradient(j)

    own = pl.ds(0, half)
    for s in range(1, n_col):
        seconds[s].wait_recv()
        part[own, :] = part[own, :] + recv2[pl.ds(s * half, half), :]
    thirds = [None] + [
        go(send(
            part.at[pl.ds(t * nd_own, nd_own)], recv3.at[pl.ds(t * nd_own, nd_own)],
            s_3.at[t], r_3.at[t], along_row[t],
        ))
        for t in range(1, chips)
    ]
    for c in l2:
        c.wait_recv()
    loss_own[2] = tree_sum([loss_own[1]] + [loss_in2[s] for s in range(1, n_col)])
    l3 = [
        go(send(loss_own.at[2], loss_in3.at[t], s_l.at[n_col + t], r_l.at[n_col + t], along_row[t]))
        for t in range(1, chips)
    ]
    total = part[pl.ds(0, nd_own), :]
    for t in range(1, chips):
        thirds[t].wait_recv()
        total = total + recv3[pl.ds(t * nd_own, nd_own), :]
    gd_ref[...] = (total * 0.0625).astype(BF16)
    for c in l3:
        c.wait_recv()
    final = tree_sum([loss_own[2]] + [loss_in3[t] for t in range(1, chips)])
    loss_ref[...] = final * (1.0 / total_q)

    for s in range(1, n_col):
        send(piece(0, 0, 0, chips), piece(s, 0, 0, chips), s_c.at[s], r_c.at[s], along_col[s]).wait_send()
    for copy in started:
        copy.wait_send()


def on_device(queries, documents, log_norms, weights, positives):
    n_row = lax.axis_size("row")
    n_col = lax.axis_size("col")
    nq, width = queries.shape
    nd_own = documents.shape[0]
    chips = n_row // 2
    nd = nd_own * n_row * n_col
    half = chips * nd_own
    sem = pltpu.SemaphoreType.DMA
    vmem = pl.BlockSpec(memory_space=pltpu.VMEM)
    hbm = pl.BlockSpec(memory_space=pl.ANY)
    gq, gd, loss = pl.pallas_call(
        functools.partial(kernel, n_row, n_col, nd_own, nq * n_row * n_col),
        out_shape=(
            jax.ShapeDtypeStruct((nq, width), BF16),
            jax.ShapeDtypeStruct((nd_own, width), BF16),
            jax.ShapeDtypeStruct((8, 128), F32),
        ),
        in_specs=[hbm, hbm, vmem, vmem, vmem],
        out_specs=(vmem, vmem, vmem),
        scratch_shapes=[
            pltpu.VMEM((nq, width), BF16),
            pltpu.VMEM((width, nq), BF16),
            pltpu.VMEM((nd, width), BF16),
            pltpu.VMEM((nd, nq), BF16),
            pltpu.VMEM((nd, width), F32),
            pltpu.VMEM((n_col * half, width), F32),
            pltpu.VMEM((n_col * half, width), F32),
            pltpu.VMEM((half, width), F32),
            pltpu.VMEM((1, nq), F32),
            pltpu.VMEM((3, 8, 128), F32),
            pltpu.VMEM((2, 8, 128), F32),
            pltpu.VMEM((n_col, 8, 128), F32),
            pltpu.VMEM((chips, 8, 128), F32),
            sem((2,)),
            sem((chips,)), sem((chips,)),
            sem((1,)), sem((1,)),
            sem((n_col,)), sem((n_col,)),
            sem((n_col,)), sem((n_col,)),
            sem((n_col,)), sem((n_col,)),
            sem((n_col,)), sem((n_col,)),
            sem((chips,)), sem((chips,)),
            sem((n_col + chips,)), sem((n_col + chips,)),
        ],
        compiler_params=pltpu.CompilerParams(
            collective_id=0, has_side_effects=True, vmem_limit_bytes=60 * 1024 * 1024
        ),
    )(
        queries, documents,
        log_norms.reshape(1, nq), weights.reshape(1, nq), positives.reshape(1, nq),
    )
    return (gq, gd, loss[0, 0])


def solution(mesh):
    placed = (
        P(("row", "col"), None),
        P(("row", "col"), None),
        P(("row", "col")),
        P(("row", "col")),
        P(("row", "col")),
    )
    return jax.shard_map(
        on_device,
        mesh=mesh,
        in_specs=placed,
        out_specs=(P(("row", "col"), None), P(("row", "col"), None), P()),
        check_vma=False,
    )
```

time: 132 us -> 37.1 us (0.28)
  blocking collectives: 47 us -> 0 us
  waiting for transfers between devices: 43 us -> 0 us
  Pallas kernels: 0 us -> 32.4 us
  matrix products: 18.5 us -> 0 us
  between operations: 15.9 us -> 0.64 us
  other arithmetic: 2.93 us -> 0 us
  local copies, waits for them, and re-layouts: 0.84 us -> 3.67 us
  starting transfers between devices: 2.21 us -> 0 us
    ppermute x16 -> x0, waiting for transfers between devices: 42.9 us -> none  [passed_along(): return lax.ppermute(block, axis, route)]
    psum x1 -> x0, blocking collectives: 37.1 us -> none  [on_device(): loss = lax.psum(local_loss, ('row', 'col')) / total_q]
    pallas_call x0 -> x1, Pallas kernels: none -> 32.4 us  [on_device(): pl.pallas_call(functools.partial(kernel, n_row, n_col, nd_own, nq * n_row...]
    dot_general x24 -> x0, matrix products: 18.5 us -> none  [the longest x8 11.4 us: visit(): jnp.dot(queries, block.T, preferred_element_type=jnp.float32) * 0.0625]
    all_gather x1 -> x0, blocking collectives: 9.88 us -> none  [on_device(): block = lax.all_gather(documents, 'col', axis=0, tiled=True)]
    convert_element_type x2 -> x0, other arithmetic: 2.24 us -> none  [the longest x1 1.37 us: on_device(): grad_documents = (grad_d * 0.0625).astype(jnp.bfloat16)]
    ppermute x16 -> x0, starting transfers between devices: 2.17 us -> none  [passed_along(): return lax.ppermute(block, axis, route)]
    unnamed x8 -> x4, local copies, waits for them, and re-layouts: 0.74 us -> 2.49 us
  transfers between devices with their start and end apart: 17 -> 0, of which waited for: 16 -> 0; matrix products, arithmetic and copies ran while one was open for 15% -> 0% of each run, Pallas kernels for 0% -> 0%
where the time goes in v1:
time: 37.1 us; the launch traced here: 36.7 us
  Pallas kernels  32.4 us (87%)
  local copies, waits for them, and re-layouts  3.67 us (10%)
  between operations  0.64 us (2%)
    pallas_call x1, Pallas kernels, on_device(): pl.pallas_call(functools.partial(kernel, n_row, n_col, nd_own, nq * n_row...  32.4 us
    unnamed x4, local copies, waits for them, and re-layouts  2.49 us
    slice x1, local copies, waits for them, and re-layouts, on_device(): return (gq, gd, loss[0, 0])  1.19 us

profile of v1, /device:TPU:0, one launch (start us, length us, event | category | flops | bytes accessed | tf_op | source)
XLA Modules:
  0.0 36.7 jit_solution(17108403237451878315)
XLA Ops:
  0.6 32.4 %shard_map.76 = (bf16[1024,256]{1,0:T(8,128)(2,1)}, bf16[32,256]{1,0:T(8,128)(2,1)}, f32[8,128]{1,0:T(8,128)}) custom-call(bf16[1024,256]{1,0:T(8,128)(2,1)} %q_hbm.1, bf16[32,256]{1,0:T(8,128)(2,1)} %d_hbm.1, f32[1,1024]{1,0:T(1,128)} %bitcast.4, f32[1,1024]{1,0:T(1,128)} %bitcast.5, s32[1,1024]{1,0:T(1,128)} %bitcast.6), custom_call_target="tpu_custom_call" | custom-call | tf_op jit(solution)/shard_map/pallas_call | solution.py:227
  33.0 1.2 %slice.3 = f32[1,1]{1,0:T(1,128)} slice(f32[8,128]{1,0:T(8,128)} %get-tuple-element.8), slice={[0:1], [0:1]} | slice | bytes 8 | tf_op jit(solution)/shard_map/slice | solution.py:267
  34.2 0.0 copy-start
  34.2 1.9 %copy.10 = bf16[1024,256]{1,0:T(8,128)(2,1)} copy(bf16[1024,256]{1,0:T(8,128)(2,1)} %get-tuple-element.12) | data formatting | bytes 1048576
  36.1 0.0 copy-done
  36.1 0.6 %copy.11 = bf16[32,256]{1,0:T(8,128)(2,1)} copy(bf16[32,256]{1,0:T(8,128)(2,1)S(1)} %copy-done) | data formatting | bytes 32768
Async XLA Ops:
  34.2 1.9 %copy-start = (bf16[32,256]{1,0:T(8,128)(2,1)S(1)}, bf16[32,256]{1,0:T(8,128)(2,1)}, u32[]{:S(2)}) copy-start(bf16[32,256]{1,0:T(8,128)(2,1)} %get-tuple-element.13) | copy-start | bytes 49156

commit v2 on v1

v2 whole, which is shorter than its diff:
```python
import functools
import math

import jax
import jax.numpy as jnp
from jax import lax
from jax.experimental import pallas as pl
from jax.experimental.pallas import tpu as pltpu
from jax.sharding import PartitionSpec as P

MESH = pl.DeviceIdType.MESH
LOG2E = math.log2(math.e)
F32 = jnp.float32
BF16 = jnp.bfloat16


def flipped(index, step, size):
    total, bit = 0, 1
    while bit < size:
        own = (index // bit) % 2
        other = (step // bit) % 2
        total = total + bit * ((own + other) % 2)
        bit *= 2
    return total


def tree_sum(parts):
    while len(parts) > 1:
        parts = [parts[i] + parts[i + 1] for i in range(0, len(parts), 2)]
    return parts[0]


def kernel(
    n_row, n_col, nd_own, total_q,
    q_hbm, d_hbm, ln_ref, w_ref, pos_ref,
    gq_ref, gd_ref, loss_ref,
    q, q_t, docs, coeffs, part, recv1, recv2, recv3, bias,
    loss_own, loss_in1, loss_in2, loss_in3,
    local_sem, s_z, r_z, s_c, r_c, s_f, r_f,
    s_1, r_1, s_2, r_2, s_3, r_3, s_l, r_l,
):
    chips = n_row // 2
    row = lax.axis_index("row")
    col = lax.axis_index("col")
    core = row % 2
    chip = row // 2
    nq, width = q.shape
    half = n_col * nd_own
    block = 2 * half

    partner = (chip * 2 + (1 - core), col)
    along_row = [None] + [(flipped(chip, t, chips) * 2 + core, col) for t in range(1, chips)]
    along_col = [None] + [(row, flipped(col, s, n_col)) for s in range(1, n_col)]

    get_d = pltpu.make_async_copy(d_hbm, docs.at[pl.ds(0, nd_own)], local_sem.at[0])
    get_d.start()
    get_q = pltpu.make_async_copy(q_hbm, q, local_sem.at[1])
    get_q.start()

    barrier = pltpu.get_barrier_semaphore()
    peers = [partner] + along_row[1:] + along_col[1:]
    for peer in peers:
        pl.semaphore_signal(barrier, inc=1, device_id=peer, device_id_type=MESH)
    get_d.wait()
    pl.semaphore_wait(barrier, len(peers))

    def send(src, dst, s_sem, r_sem, peer):
        return pltpu.make_async_remote_copy(
            src_ref=src, dst_ref=dst, send_sem=s_sem, recv_sem=r_sem,
            device_id=peer, device_id_type=MESH,
        )

    def piece(t, k, s, count=1):
        return docs.at[pl.ds(t * block + k * half + s * nd_own, count * nd_own)]

    started = []

    def go(copy):
        copy.start()
        started.append(copy)
        return copy

    def from_row(t):
        return send(piece(0, 0, 0), piece(t, 0, 0), s_z.at[t], r_z.at[t], along_row[t])

    def over_col(t):
        for s in range(1, n_col):
            send(piece(t, 0, 0), piece(t, 0, s), s_c.at[t], r_c.at[t], along_col[s]).start()

    def all_over_col(t):
        others = piece(t, 0, 1, n_col - 1)
        return send(others, others, s_c.at[t], r_c.at[t], along_col[1])

    fwd = {}

    def to_partner(t):
        all_over_col(t).wait_recv()
        fwd[t] = go(send(piece(t, 0, 0, n_col), piece(t, 1, 0, n_col), s_f.at[t], r_f.at[t], partner))

    order = [0] + list(range(chips - 1, 0, -1))
    for t in order[1:]:
        go(from_row(t))
    over_col(0)
    bias[...] = ln_ref[...] * LOG2E - jnp.log2(w_ref[...])
    get_q.wait()
    q_t[...] = q[...].T
    to_partner(0)
    for t in order[1:]:
        from_row(t).wait_recv()
        over_col(t)

    rows_per = math.gcd(block, 256)
    pieces = rows_per // nd_own
    n_sub = block // rows_per
    iota = lax.broadcasted_iota(jnp.int32, (nd_own, nq), 0)

    def scores_of(t, sub, acc):
        base = pl.multiple_of(t * block + sub * rows_per, rows_per)
        d = docs[pl.ds(base, rows_per), :]
        sc = jnp.dot(d, q_t[...], preferred_element_type=F32)
        owner_chip = flipped(chip, t, chips)
        for p in range(pieces):
            at = sub * pieces + p
            k, s = at // n_col, at % n_col
            owner_row = owner_chip * 2 + (core + k) % 2
            first = (owner_row * n_col + flipped(col, s, n_col)) * nd_own
            x = sc[p * nd_own:(p + 1) * nd_own, :]
            hit_w = jnp.where(pos_ref[...] - first == iota, w_ref[...], 0.0)
            co = jnp.exp2(x * (0.0625 * LOG2E) - bias[...]) - hit_w
            coeffs[pl.ds(base + p * nd_own, nd_own), :] = co.astype(BF16)
            acc = acc + hit_w * x
        part[pl.ds(base, rows_per), :] = jnp.dot(
            coeffs[pl.ds(base, rows_per), :], q[...], preferred_element_type=F32
        )
        return acc

    def pair_copy(t):
        return send(
            part.at[pl.ds(t * block + half, half)], recv1.at[pl.ds(t * half, half)],
            s_1.at[t], r_1.at[t], partner,
        )

    def reduce_pair(t):
        pair_copy(t).wait_recv()
        own = pl.ds(t * block, half)
        part[own, :] = part[own, :] + recv1[pl.ds(t * half, half), :]
        for s in range(1, n_col):
            send(
                part.at[pl.ds(t * block + s * nd_own, nd_own)],
                recv2.at[pl.ds(t * half + s * nd_own, nd_own)],
                s_2.at[t], r_2.at[t], along_col[s],
            ).start()

    def all_col_sums(t):
        rest = (n_col - 1) * nd_own
        return send(
            part.at[pl.ds(t * block + nd_own, rest)],
            recv2.at[pl.ds(t * half + nd_own, rest)],
            s_2.at[t], r_2.at[t], along_col[1],
        )

    def row_copy(t):
        return send(
            part.at[pl.ds(t * block, nd_own)], recv3.at[pl.ds(t * nd_own, nd_own)],
            s_3.at[t], r_3.at[t], along_row[t],
        )

    def reduce_col(t):
        all_col_sums(t).wait_recv()
        total = part[pl.ds(t * block, nd_own), :]
        for s in range(1, n_col):
            total = total + recv2[pl.ds(t * half + s * nd_own, nd_own), :]
        part[pl.ds(t * block, nd_own), :] = total
        if t:
            go(row_copy(t))

    hit_sum = jnp.zeros((nd_own, nq), F32)
    for i, t in enumerate(order):
        fwd[t].wait_recv()
        if i + 1 < chips and i == 0:
            to_partner(order[1])
        if n_sub == 1:
            hit_sum = scores_of(t, 0, hit_sum)
        else:
            hit_sum = lax.fori_loop(0, n_sub, functools.partial(scores_of, t), hit_sum)
        go(pair_copy(t))
        if i + 2 < chips:
            to_partner(order[i + 2])
        if i >= 1:
            reduce_pair(order[i - 1])
        if i >= 2:
            reduce_col(order[i - 2])

    terms = w_ref[...] * ln_ref[...] - 0.0625 * jnp.sum(hit_sum, axis=0, keepdims=True)
    loss_own[0] = jnp.broadcast_to(jnp.sum(terms, axis=1, keepdims=True), (8, 128))
    l1 = go(send(loss_own.at[0], loss_in1.at[1], s_l.at[0], r_l.at[0], partner))

    d_t = docs[...].T
    chunk = math.gcd(nq, 256)
    n_chunks = nq // chunk

    def query_gradient(j):
        at = slice(j * chunk, (j + 1) * chunk)
        g = jnp.dot(d_t, coeffs[:, at], preferred_element_type=F32)
        gq_ref[at, :] = (g.T * 0.0625).astype(BF16)

    reduce_pair(order[-1])
    l1.wait_recv()
    loss_own[1] = loss_own[0] + loss_in1[1]
    l2 = [go(send(loss_own.at[1], loss_in2.at[s], s_l.at[s], r_l.at[s], along_col[s])) for s in range(1, n_col)]
    if chips > 1:
        reduce_col(order[-2])
    for j in range(n_chunks):
        query_gradient(j)
    reduce_col(order[-1])
    for c in l2:
        c.wait_recv()
    loss_own[2] = tree_sum([loss_own[1]] + [loss_in2[s] for s in range(1, n_col)])
    l3 = [
        go(send(loss_own.at[2], loss_in3.at[t], s_l.at[n_col + t], r_l.at[n_col + t], along_row[t]))
        for t in range(1, chips)
    ]
    total = part[pl.ds(0, nd_own), :]
    for t in order[1:]:
        row_copy(t).wait_recv()
        total = total + recv3[pl.ds(t * nd_own, nd_own), :]
    gd_ref[...] = (total * 0.0625).astype(BF16)
    for c in l3:
        c.wait_recv()
    final = tree_sum([loss_own[2]] + [loss_in3[t] for t in range(1, chips)])
    loss_ref[...] = final * (1.0 / total_q)

    for t in range(chips):
        all_over_col(t).wait_send()
        all_col_sums(t).wait_send()
    for copy in started:
        copy.wait_send()


def on_device(queries, documents, log_norms, weights, positives):
    n_row = lax.axis_size("row")
    n_col = lax.axis_size("col")
    nq, width = queries.shape
    nd_own = documents.shape[0]
    chips = n_row // 2
    nd = nd_own * n_row * n_col
    half = n_col * nd_own
    sem = pltpu.SemaphoreType.DMA
    vmem = pl.BlockSpec(memory_space=pltpu.VMEM)
    hbm = pl.BlockSpec(memory_space=pl.ANY)
    gq, gd, loss = pl.pallas_call(
        functools.partial(kernel, n_row, n_col, nd_own, nq * n_row * n_col),
        out_shape=(
            pltpu.VMEM((nq, width), BF16),
            pltpu.VMEM((nd_own, width), BF16),
            pltpu.VMEM((8, 128), F32),
        ),
        in_specs=[hbm, hbm, vmem, vmem, vmem],
        out_specs=(vmem, vmem, vmem),
        scratch_shapes=[
            pltpu.VMEM((nq, width), BF16),
            pltpu.VMEM((width, nq), BF16),
            pltpu.VMEM((nd, width), BF16),
            pltpu.VMEM((nd, nq), BF16),
            pltpu.VMEM((nd, width), F32),
            pltpu.VMEM((chips * half, width), F32),
            pltpu.VMEM((chips * half, width), F32),
            pltpu.VMEM((chips * nd_own, width), F32),
            pltpu.VMEM((1, nq), F32),
            pltpu.VMEM((3, 8, 128), F32),
            pltpu.VMEM((2, 8, 128), F32),
            pltpu.VMEM((n_col, 8, 128), F32),
            pltpu.VMEM((chips, 8, 128), F32),
            sem((2,)),
            sem((chips,)), sem((chips,)),
            sem((chips,)), sem((chips,)),
            sem((chips,)), sem((chips,)),
            sem((chips,)), sem((chips,)),
            sem((chips,)), sem((chips,)),
            sem((chips,)), sem((chips,)),
            sem((n_col + chips,)), sem((n_col + chips,)),
        ],
        compiler_params=pltpu.CompilerParams(
            collective_id=0, has_side_effects=True, vmem_limit_bytes=60 * 1024 * 1024
        ),
    )(
        queries, documents,
        log_norms.reshape(1, nq), weights.reshape(1, nq), positives.reshape(1, nq),
    )
    return (gq, gd, loss[0, 0])


def solution(mesh):
    placed = (
        P(("row", "col"), None),
        P(("row", "col"), None),
        P(("row", "col")),
        P(("row", "col")),
        P(("row", "col")),
    )
    return jax.shard_map(
        on_device,
        mesh=mesh,
        in_specs=placed,
        out_specs=(P(("row", "col"), None), P(("row", "col"), None), P()),
        check_vma=False,
    )
```

time: 37.1 us -> 32.6 us (0.88)
  Pallas kernels: 32.4 us -> 29.8 us
  local copies, waits for them, and re-layouts: 3.67 us -> 1.91 us
    pallas_call x1, Pallas kernels: 32.4 us -> 29.8 us  [on_device(): pl.pallas_call(functools.partial(kernel, n_row, n_col, nd_own, nq * n_row...]
    unnamed x4 -> x2, local copies, waits for them, and re-layouts: 2.49 us -> 1.4 us
    slice x1, local copies, waits for them, and re-layouts: 1.19 us -> 0.51 us  [on_device(): return (gq, gd, loss[0, 0])]
where the time goes in v2:
time: 32.6 us; the launch traced here: 32.3 us
  Pallas kernels  29.8 us (91%)
  local copies, waits for them, and re-layouts  1.91 us (6%)
  between operations  0.64 us (2%)
    pallas_call x1, Pallas kernels, on_device(): pl.pallas_call(functools.partial(kernel, n_row, n_col, nd_own, nq * n_row...  29.8 us
    unnamed x2, local copies, waits for them, and re-layouts  1.4 us

profile of v2, /device:TPU:0, one launch (start us, length us, event | category | flops | bytes accessed | tf_op | source)
XLA Modules:
  0.0 32.3 jit_solution(14856308533914636705)
XLA Ops:
  0.6 29.8 %shard_map.76 = (bf16[1024,256]{1,0:T(8,128)(2,1)S(1)}, bf16[32,256]{1,0:T(8,128)(2,1)S(1)}, f32[8,128]{1,0:T(8,128)S(1)}) custom-call(bf16[1024,256]{1,0:T(8,128)(2,1)} %q_hbm.1, bf16[32,256]{1,0:T(8,128)(2,1)} %d_hbm.1, f32[1,1024]{1,0:T(1,128)} %bitcast.4, f32[1,1024]{1,0:T(1,128)} %bitcast.5, s32[1,1024]{1,0:T(1,128)} %bitcast.6), custom_call_target="tpu_custom_call" | custom-call | tf_op jit(solution)/shard_map/pallas_call | solution.py:251
  30.4 0.5 %slice.3 = f32[1,1]{1,0:T(1,128)} slice(f32[8,128]{1,0:T(8,128)S(1)} %get-tuple-element.8), slice={[0:1], [0:1]} | slice | bytes 8 | tf_op jit(solution)/shard_map/slice | solution.py:290
  30.9 0.8 %copy.10 = bf16[1024,256]{1,0:T(8,128)(2,1)} copy(bf16[1024,256]{1,0:T(8,128)(2,1)S(1)} %get-tuple-element.9) | data formatting | bytes 1048576
  31.7 0.6 %copy.11 = bf16[32,256]{1,0:T(8,128)(2,1)} copy(bf16[32,256]{1,0:T(8,128)(2,1)S(1)} %get-tuple-element.10) | data formatting | bytes 32768

commit v3 on v2

v3 whole, which is shorter than its diff:
```python
import functools
import math

import jax
import jax.numpy as jnp
from jax import lax
from jax.experimental import pallas as pl
from jax.experimental.pallas import tpu as pltpu
from jax.sharding import PartitionSpec as P

MESH = pl.DeviceIdType.MESH
LOG2E = math.log2(math.e)
F32 = jnp.float32
BF16 = jnp.bfloat16


def flipped(index, step, size):
    total, bit = 0, 1
    while bit < size:
        own = (index // bit) % 2
        other = (step // bit) % 2
        total = total + bit * ((own + other) % 2)
        bit *= 2
    return total


def tree_sum(parts):
    while len(parts) > 1:
        parts = [parts[i] + parts[i + 1] for i in range(0, len(parts), 2)]
    return parts[0]


def kernel(
    n_row, n_col, nd_own, total_q,
    q_hbm, d_hbm, ln_ref, w_ref, pos_ref,
    gq_ref, gd_ref, loss_ref,
    q, q_t, docs, coeffs, part, recv2, recv3, bias, w2, pos2, ln2,
    gq_own, gq_out, gq_in, loss_own, loss_in,
    local_sem, s_z, r_z, s_c, r_c, s_2, r_2, s_3, r_3, s_l, r_l, s_q, r_q, s_g, r_g,
):
    chips = n_row // 2
    row = lax.axis_index("row")
    col = lax.axis_index("col")
    core = row % 2
    chip = row // 2
    nq, width = q_hbm.shape
    block = n_col * nd_own

    partner = (chip * 2 + (1 - core), col)
    along_row = [None] + [(flipped(chip, t, chips) * 2 + core, col) for t in range(1, chips)]
    along_col = [None] + [(row, flipped(col, s, n_col)) for s in range(1, n_col)]

    mine, theirs = pl.ds(0, nq), pl.ds(nq, nq)
    get_d = pltpu.make_async_copy(d_hbm, docs.at[pl.ds(0, nd_own)], local_sem.at[0])
    get_d.start()
    get_q = pltpu.make_async_copy(q_hbm, q.at[mine], local_sem.at[1])
    get_q.start()

    barrier = pltpu.get_barrier_semaphore()
    peers = [partner] + along_row[1:] + along_col[1:]
    for peer in peers:
        pl.semaphore_signal(barrier, inc=1, device_id=peer, device_id_type=MESH)
    get_d.wait()
    pl.semaphore_wait(barrier, len(peers))

    def send(src, dst, s_sem, r_sem, peer):
        return pltpu.make_async_remote_copy(
            src_ref=src, dst_ref=dst, send_sem=s_sem, recv_sem=r_sem,
            device_id=peer, device_id_type=MESH,
        )

    def piece(t, s, count=1):
        return docs.at[pl.ds(t * block + s * nd_own, count * nd_own)]

    started = []

    def go(copy):
        copy.start()
        started.append(copy)
        return copy

    def from_row(t):
        return send(piece(0, 0), piece(t, 0), s_z.at[t], r_z.at[t], along_row[t])

    def over_col(t):
        for s in range(1, n_col):
            send(piece(t, 0), piece(t, s), s_c.at[t], r_c.at[t], along_col[s]).start()

    def all_over_col(t):
        others = piece(t, 1, n_col - 1)
        return send(others, others, s_c.at[t], r_c.at[t], along_col[1])

    order = [0] + list(range(chips - 1, 0, -1))
    for t in order[1:]:
        go(from_row(t))
    over_col(0)

    shared = []
    for i, (own, both) in enumerate(((ln_ref, ln2), (w_ref, w2), (pos_ref, pos2))):
        shared.append(go(send(own, both.at[:, theirs], s_q.at[i], r_q.at[i], partner)))
        both[:, mine] = own[...]
    get_q.wait()
    q_copy = go(send(q.at[mine], q.at[theirs], s_q.at[3], r_q.at[3], partner))
    q_t[:, mine] = q[mine, :].T
    for c in shared:
        c.wait_recv()
    bias[...] = ln2[...] * LOG2E - jnp.log2(w2[...])
    q_copy.wait_recv()
    q_t[:, theirs] = q[theirs, :].T
    for t in order[1:]:
        from_row(t).wait_recv()
        over_col(t)

    iota = lax.broadcasted_iota(jnp.int32, (nd_own, 2 * nq), 0)

    def scores_of(t, acc):
        rows = pl.ds(t * block, block)
        sc = jnp.dot(docs[rows, :], q_t[...], preferred_element_type=F32)
        owner_row = flipped(chip, t, chips) * 2 + core
        for s in range(n_col):
            first = (owner_row * n_col + flipped(col, s, n_col)) * nd_own
            x = sc[s * nd_own:(s + 1) * nd_own, :]
            hit_w = jnp.where(pos2[...] - first == iota, w2[...], 0.0)
            co = jnp.exp2(x * (0.0625 * LOG2E) - bias[...]) - hit_w
            coeffs[pl.ds(t * block + s * nd_own, nd_own), :] = co.astype(BF16)
            acc = acc + jnp.sum((hit_w * x).reshape(nd_own // 8, 8, 2 * nq), axis=0)
        part[rows, :] = jnp.dot(coeffs[rows, :], q[...], preferred_element_type=F32)
        return acc

    def send_col(t):
        for s in range(1, n_col):
            at = pl.ds(t * block + s * nd_own, nd_own)
            send(part.at[at], recv2.at[at], s_2.at[t], r_2.at[t], along_col[s]).start()

    def all_col_sums(t):
        at = pl.ds(t * block + nd_own, (n_col - 1) * nd_own)
        return send(part.at[at], recv2.at[at], s_2.at[t], r_2.at[t], along_col[1])

    def row_copy(t):
        return send(
            part.at[pl.ds(t * block, nd_own)], recv3.at[pl.ds(t * nd_own, nd_own)],
            s_3.at[t], r_3.at[t], along_row[t],
        )

    def reduce_col(t):
        all_col_sums(t).wait_recv()
        total = part[pl.ds(t * block, nd_own), :]
        for s in range(1, n_col):
            total = total + recv2[pl.ds(t * block + s * nd_own, nd_own), :]
        part[pl.ds(t * block, nd_own), :] = total
        if t:
            go(row_copy(t))

    hit_sum = jnp.zeros((8, 2 * nq), F32)
    for i, t in enumerate(order):
        all_over_col(t).wait_recv()
        hit_sum = scores_of(t, hit_sum)
        send_col(t)
        if i >= 2:
            reduce_col(order[i - 2])

    hits = jnp.sum(jnp.sum(hit_sum, axis=0, keepdims=True), axis=1, keepdims=True)
    known = jnp.sum(w_ref[...] * ln_ref[...], axis=1, keepdims=True)
    loss_own[0] = jnp.broadcast_to(known - 0.0625 * hits, (8, 128))
    l_row = [
        go(send(loss_own.at[0], loss_in.at[t], s_l.at[t], r_l.at[t], along_row[t]))
        for t in range(1, chips)
    ]

    d_t = docs[...].T
    chunk = math.gcd(nq, 256)
    n_chunks = nq // chunk

    def query_gradient(first, j):
        at = pl.ds(first + j * chunk, chunk)
        return jnp.dot(d_t, coeffs[:, at], preferred_element_type=F32)

    g_copies = []
    for j in range(n_chunks):
        gq_out[j] = query_gradient(nq, j)
        g_copies.append(go(send(gq_out.at[j], gq_in.at[j], s_g.at[j], r_g.at[j], partner)))
    if chips > 1:
        reduce_col(order[-2])
    for j in range(n_chunks // 2):
        gq_own[j] = query_gradient(0, j)
    for c in l_row:
        c.wait_recv()
    loss_own[1] = tree_sum([loss_own[0]] + [loss_in[t] for t in range(1, chips)])
    l_col = [
        go(send(loss_own.at[1], loss_in.at[chips + s], s_l.at[chips + s], r_l.at[chips + s], along_col[s]))
        for s in range(1, n_col)
    ]
    reduce_col(order[-1])
    for j in range(n_chunks // 2, n_chunks):
        gq_own[j] = query_gradient(0, j)
    for j in range(n_chunks):
        g_copies[j].wait_recv()
        gq_ref[pl.ds(j * chunk, chunk), :] = ((gq_own[j] + gq_in[j]).T * 0.0625).astype(BF16)
    for c in l_col:
        c.wait_recv()
    loss_own[2] = tree_sum([loss_own[1]] + [loss_in[chips + s] for s in range(1, n_col)])
    l_pair = go(send(loss_own.at[2], loss_in.at[0], s_l.at[0], r_l.at[0], partner))
    total = part[pl.ds(0, nd_own), :]
    for t in order[1:]:
        row_copy(t).wait_recv()
        total = total + recv3[pl.ds(t * nd_own, nd_own), :]
    gd_ref[...] = (total * 0.0625).astype(BF16)
    l_pair.wait_recv()
    loss_ref[...] = (loss_own[2] + loss_in[0]) * (1.0 / total_q)

    for t in range(chips):
        all_over_col(t).wait_send()
        all_col_sums(t).wait_send()
    for copy in started:
        copy.wait_send()


def on_device(queries, documents, log_norms, weights, positives):
    n_row = lax.axis_size("row")
    n_col = lax.axis_size("col")
    nq, width = queries.shape
    nd_own = documents.shape[0]
    chips = n_row // 2
    nd = chips * n_col * nd_own
    chunk = math.gcd(nq, 256)
    n_chunks = nq // chunk
    sem = pltpu.SemaphoreType.DMA
    vmem = pl.BlockSpec(memory_space=pltpu.VMEM)
    hbm = pl.BlockSpec(memory_space=pl.ANY)
    gq, gd, loss = pl.pallas_call(
        functools.partial(kernel, n_row, n_col, nd_own, nq * n_row * n_col),
        out_shape=(
            pltpu.VMEM((nq, width), BF16),
            pltpu.VMEM((nd_own, width), BF16),
            pltpu.VMEM((8, 128), F32),
        ),
        in_specs=[hbm, hbm, vmem, vmem, vmem],
        out_specs=(vmem, vmem, vmem),
        scratch_shapes=[
            pltpu.VMEM((2 * nq, width), BF16),
            pltpu.VMEM((width, 2 * nq), BF16),
            pltpu.VMEM((nd, width), BF16),
            pltpu.VMEM((nd, 2 * nq), BF16),
            pltpu.VMEM((nd, width), F32),
            pltpu.VMEM((nd, width), F32),
            pltpu.VMEM((chips * nd_own, width), F32),
            pltpu.VMEM((1, 2 * nq), F32),
            pltpu.VMEM((1, 2 * nq), F32),
            pltpu.VMEM((1, 2 * nq), jnp.int32),
            pltpu.VMEM((1, 2 * nq), F32),
            pltpu.VMEM((n_chunks, width, chunk), F32),
            pltpu.VMEM((n_chunks, width, chunk), F32),
            pltpu.VMEM((n_chunks, width, chunk), F32),
            pltpu.VMEM((3, 8, 128), F32),
            pltpu.VMEM((chips + n_col, 8, 128), F32),
            sem((2,)),
        ] + [sem((chips,))] * 8 + [sem((chips + n_col,))] * 2 + [sem((4,))] * 2 + [sem((n_chunks,))] * 2,
        compiler_params=pltpu.CompilerParams(
            collective_id=0, has_side_effects=True, vmem_limit_bytes=60 * 1024 * 1024
        ),
    )(
        queries, documents,
        log_norms.reshape(1, nq), weights.reshape(1, nq), positives.reshape(1, nq),
    )
    return (gq, gd, loss[0, 0])


def solution(mesh):
    placed = (
        P(("row", "col"), None),
        P(("row", "col"), None),
        P(("row", "col")),
        P(("row", "col")),
        P(("row", "col")),
    )
    return jax.shard_map(
        on_device,
        mesh=mesh,
        in_specs=placed,
        out_specs=(P(("row", "col"), None), P(("row", "col"), None), P()),
        check_vma=False,
    )
```

time: 32.6 us -> 29.6 us (0.908)
  Pallas kernels: 29.8 us -> 26.8 us
    pallas_call x1, Pallas kernels: 29.8 us -> 26.8 us  [on_device(): pl.pallas_call(functools.partial(kernel, n_row, n_col, nd_own, nq * n_row...]
where the time goes in v3:
time: 29.6 us; the launch traced here: 29.3 us
  Pallas kernels  26.8 us (91%)
  local copies, waits for them, and re-layouts  1.91 us (6%)
  between operations  0.64 us (2%)
    pallas_call x1, Pallas kernels, on_device(): pl.pallas_call(functools.partial(kernel, n_row, n_col, nd_own, nq * n_row...  26.8 us
    unnamed x2, local copies, waits for them, and re-layouts  1.4 us

profile of v3, /device:TPU:0, one launch (start us, length us, event | category | flops | bytes accessed | tf_op | source)
XLA Modules:
  0.0 29.3 jit_solution(11604412105394167075)
XLA Ops:
  0.6 26.8 %shard_map.76 = (bf16[1024,256]{1,0:T(8,128)(2,1)S(1)}, bf16[32,256]{1,0:T(8,128)(2,1)S(1)}, f32[8,128]{1,0:T(8,128)S(1)}) custom-call(bf16[1024,256]{1,0:T(8,128)(2,1)} %q_hbm.1, bf16[32,256]{1,0:T(8,128)(2,1)} %d_hbm.1, f32[1,1024]{1,0:T(1,128)} %bitcast.4, f32[1,1024]{1,0:T(1,128)} %bitcast.5, s32[1,1024]{1,0:T(1,128)} %bitcast.6), custom_call_target="tpu_custom_call" | custom-call | tf_op jit(solution)/shard_map/pallas_call | solution.py:230
  27.4 0.5 %slice.3 = f32[1,1]{1,0:T(1,128)} slice(f32[8,128]{1,0:T(8,128)S(1)} %get-tuple-element.8), slice={[0:1], [0:1]} | slice | bytes 8 | tf_op jit(solution)/shard_map/slice | solution.py:265
  27.9 0.8 %copy.10 = bf16[1024,256]{1,0:T(8,128)(2,1)} copy(bf16[1024,256]{1,0:T(8,128)(2,1)S(1)} %get-tuple-element.9) | data formatting | bytes 1048576
  28.7 0.6 %copy.11 = bf16[32,256]{1,0:T(8,128)(2,1)} copy(bf16[32,256]{1,0:T(8,128)(2,1)S(1)} %get-tuple-element.10) | data formatting | bytes 32768

commit v4 on v3

--- a/solution.py
+++ b/solution.py
@@ -47,6 +47,7 @@
     block = n_col * nd_own
 
     partner = (chip * 2 + (1 - core), col)
+    across = [(flipped(chip, t, chips) * 2 + (1 - core), col) for t in range(1, chips)]
     along_row = [None] + [(flipped(chip, t, chips) * 2 + core, col) for t in range(1, chips)]
     along_col = [None] + [(row, flipped(col, s, n_col)) for s in range(1, n_col)]
 
@@ -57,7 +58,7 @@
     get_q.start()
 
     barrier = pltpu.get_barrier_semaphore()
-    peers = [partner] + along_row[1:] + along_col[1:]
+    peers = [partner] + along_row[1:] + across + along_col[1:]
     for peer in peers:
         pl.semaphore_signal(barrier, inc=1, device_id=peer, device_id_type=MESH)
     get_d.wait()
@@ -102,18 +103,17 @@
     get_q.wait()
     q_copy = go(send(q.at[mine], q.at[theirs], s_q.at[3], r_q.at[3], partner))
     q_t[:, mine] = q[mine, :].T
+    for t in order[1:]:
+        from_row(t).wait_recv()
+        over_col(t)
     for c in shared:
         c.wait_recv()
     bias[...] = ln2[...] * LOG2E - jnp.log2(w2[...])
     q_copy.wait_recv()
     q_t[:, theirs] = q[theirs, :].T
-    for t in order[1:]:
-        from_row(t).wait_recv()
-        over_col(t)
-
     iota = lax.broadcasted_iota(jnp.int32, (nd_own, 2 * nq), 0)
 
-    def scores_of(t, acc):
+    def coeffs_of(t, acc):
         rows = pl.ds(t * block, block)
         sc = jnp.dot(docs[rows, :], q_t[...], preferred_element_type=F32)
         owner_row = flipped(chip, t, chips) * 2 + core
@@ -124,8 +124,11 @@
             co = jnp.exp2(x * (0.0625 * LOG2E) - bias[...]) - hit_w
             coeffs[pl.ds(t * block + s * nd_own, nd_own), :] = co.astype(BF16)
             acc = acc + jnp.sum((hit_w * x).reshape(nd_own // 8, 8, 2 * nq), axis=0)
+        return acc
+
+    def document_sums(t):
+        rows = pl.ds(t * block, block)
         part[rows, :] = jnp.dot(coeffs[rows, :], q[...], preferred_element_type=F32)
-        return acc
 
     def send_col(t):
         for s in range(1, n_col):
@@ -152,20 +155,23 @@
             go(row_copy(t))
 
     hit_sum = jnp.zeros((8, 2 * nq), F32)
+    known = jnp.sum(w_ref[...] * ln_ref[...], axis=1, keepdims=True)
+    row_group = [partner] + [peer for pair in zip(along_row[1:], across) for peer in pair]
+    l_row = []
     for i, t in enumerate(order):
         all_over_col(t).wait_recv()
-        hit_sum = scores_of(t, hit_sum)
+        hit_sum = coeffs_of(t, hit_sum)
+        if i == chips - 1:
+            hits = jnp.sum(jnp.sum(hit_sum, axis=0, keepdims=True), axis=1, keepdims=True)
+            loss_own[0] = jnp.broadcast_to(known - 0.0625 * hits, (8, 128))
+            for m, peer in reversed(list(enumerate(row_group, 1))):
+                l_row.append(
+                    go(send(loss_own.at[0], loss_in.at[m], s_l.at[m], r_l.at[m], peer))
+                )
+        document_sums(t)
         send_col(t)
         if i >= 2:
             reduce_col(order[i - 2])
-
-    hits = jnp.sum(jnp.sum(hit_sum, axis=0, keepdims=True), axis=1, keepdims=True)
-    known = jnp.sum(w_ref[...] * ln_ref[...], axis=1, keepdims=True)
-    loss_own[0] = jnp.broadcast_to(known - 0.0625 * hits, (8, 128))
-    l_row = [
-        go(send(loss_own.at[0], loss_in.at[t], s_l.at[t], r_l.at[t], along_row[t]))
-        for t in range(1, chips)
-    ]
 
     d_t = docs[...].T
     chunk = math.gcd(nq, 256)
@@ -185,9 +191,9 @@
         gq_own[j] = query_gradient(0, j)
     for c in l_row:
         c.wait_recv()
-    loss_own[1] = tree_sum([loss_own[0]] + [loss_in[t] for t in range(1, chips)])
+    loss_own[1] = tree_sum([loss_own[0]] + [loss_in[m] for m in range(1, n_row)])
     l_col = [
-        go(send(loss_own.at[1], loss_in.at[chips + s], s_l.at[chips + s], r_l.at[chips + s], along_col[s]))
+        go(send(loss_own.at[1], loss_in.at[n_row + s], s_l.at[n_row + s], r_l.at[n_row + s], along_col[s]))
         for s in range(1, n_col)
     ]
     reduce_col(order[-1])
@@ -196,17 +202,14 @@
     for j in range(n_chunks):
         g_copies[j].wait_recv()
         gq_ref[pl.ds(j * chunk, chunk), :] = ((gq_own[j] + gq_in[j]).T * 0.0625).astype(BF16)
-    for c in l_col:
-        c.wait_recv()
-    loss_own[2] = tree_sum([loss_own[1]] + [loss_in[chips + s] for s in range(1, n_col)])
-    l_pair = go(send(loss_own.at[2], loss_in.at[0], s_l.at[0], r_l.at[0], partner))
     total = part[pl.ds(0, nd_own), :]
     for t in order[1:]:
         row_copy(t).wait_recv()
         total = total + recv3[pl.ds(t * nd_own, nd_own), :]
     gd_ref[...] = (total * 0.0625).astype(BF16)
-    l_pair.wait_recv()
-    loss_ref[...] = (loss_own[2] + loss_in[0]) * (1.0 / total_q)
+    for c in l_col:
+        c.wait_recv()
+    loss_ref[...] = tree_sum([loss_own[1]] + [loss_in[n_row + s] for s in range(1, n_col)]) * (1.0 / total_q)
 
     for t in range(chips):
         all_over_col(t).wait_send()
@@ -251,10 +254,10 @@
             pltpu.VMEM((n_chunks, width, chunk), F32),
             pltpu.VMEM((n_chunks, width, chunk), F32),
             pltpu.VMEM((n_chunks, width, chunk), F32),
-            pltpu.VMEM((3, 8, 128), F32),
-            pltpu.VMEM((chips + n_col, 8, 128), F32),
+            pltpu.VMEM((2, 8, 128), F32),
+            pltpu.VMEM((n_row + n_col, 8, 128), F32),
             sem((2,)),
-        ] + [sem((chips,))] * 8 + [sem((chips + n_col,))] * 2 + [sem((4,))] * 2 + [sem((n_chunks,))] * 2,
+        ] + [sem((chips,))] * 8 + [sem((n_row + n_col,))] * 2 + [sem((4,))] * 2 + [sem((n_chunks,))] * 2,
         compiler_params=pltpu.CompilerParams(
             collective_id=0, has_side_effects=True, vmem_limit_bytes=60 * 1024 * 1024
         ),

time: 29.6 us -> 27.3 us (0.922)
  Pallas kernels: 26.8 us -> 24.5 us
    pallas_call x1, Pallas kernels: 26.8 us -> 24.5 us  [on_device(): pl.pallas_call(functools.partial(kernel, n_row, n_col, nd_own, nq * n_row...]
where the time goes in v4:
time: 27.3 us; the launch traced here: 27 us
  Pallas kernels  24.5 us (90%)
  local copies, waits for them, and re-layouts  1.91 us (7%)
  between operations  0.64 us (2%)
    pallas_call x1, Pallas kernels, on_device(): pl.pallas_call(functools.partial(kernel, n_row, n_col, nd_own, nq * n_row...  24.5 us
    unnamed x2, local copies, waits for them, and re-layouts  1.4 us

profile of v4, /device:TPU:0, one launch (start us, length us, event | category | flops | bytes accessed | tf_op | source)
XLA Modules:
  0.0 27.0 jit_solution(1325204673600329731)
XLA Ops:
  0.6 24.5 %shard_map.76 = (bf16[1024,256]{1,0:T(8,128)(2,1)S(1)}, bf16[32,256]{1,0:T(8,128)(2,1)S(1)}, f32[8,128]{1,0:T(8,128)S(1)}) custom-call(bf16[1024,256]{1,0:T(8,128)(2,1)} %q_hbm.1, bf16[32,256]{1,0:T(8,128)(2,1)} %d_hbm.1, f32[1,1024]{1,0:T(1,128)} %bitcast.4, f32[1,1024]{1,0:T(1,128)} %bitcast.5, s32[1,1024]{1,0:T(1,128)} %bitcast.6), custom_call_target="tpu_custom_call" | custom-call | tf_op jit(solution)/shard_map/pallas_call | solution.py:233
  25.1 0.5 %slice.3 = f32[1,1]{1,0:T(1,128)} slice(f32[8,128]{1,0:T(8,128)S(1)} %get-tuple-element.8), slice={[0:1], [0:1]} | slice | bytes 8 | tf_op jit(solution)/shard_map/slice | solution.py:268
  25.6 0.8 %copy.10 = bf16[1024,256]{1,0:T(8,128)(2,1)} copy(bf16[1024,256]{1,0:T(8,128)(2,1)S(1)} %get-tuple-element.9) | data formatting | bytes 1048576
  26.4 0.6 %copy.11 = bf16[32,256]{1,0:T(8,128)(2,1)} copy(bf16[32,256]{1,0:T(8,128)(2,1)S(1)} %get-tuple-element.10) | data formatting | bytes 32768
